TPU v7x, 768 devices: a whole 4x8x12 slice. The times are simulated.
768 devices in a mesh: gx: 24 (over x, z_hi, core), gy: 8 (over y), gz: 4 (over z_lo).
Axes of the slice: x: 4, y: 8, z: 12 (z_hi: 3, z_lo: 4; z = z_hi * 4 + z_lo), core: 2. Of those that a mesh axis runs over, the one named last changes fastest.
Arguments:
- fields: float32 [32, 192, 64, 512], P(None, 'gx', 'gy', 'gz'), may hold values from -8 to 8
- strength: float32 [32], replicated, may hold values from 0.3 to 1
Outputs:
- filtered: float32 [32, 192, 64, 512], P(None, 'gx', 'gy', 'gz')
All inputs are finite; a program needn't handle non-finite values.
Results may differ from a plain program's by a relative error of at most 0.00002.
Values sent between devices are 32-bit elements; how exact they have to be, the bound alone decides.
A program may use at most 64 MiB of HBM per device.

v0:
```python
import jax
import jax.numpy as jnp
from jax import lax
from jax.sharding import PartitionSpec as P

filter_weights = [1.0, -10.0, 45.0, -120.0, 210.0, -252.0, 210.0, -120.0, 45.0, -10.0, 1.0]


def with_halo(cells, sides, width):
    for axis, dim in sides:
        count = lax.axis_size(axis)
        head = lax.slice_in_dim(cells, 0, width, axis=dim)
        tail = lax.slice_in_dim(cells, cells.shape[dim] - width, cells.shape[dim], axis=dim)
        cells = jnp.concatenate(
            [
                lax.ppermute(tail, axis, [(i, (i + 1) % count) for i in range(count)]),
                cells,
                lax.ppermute(head, axis, [((i + 1) % count, i) for i in range(count)]),
            ],
            axis=dim,
        )
    return cells


def difference_along(padded, axis, length, starts):
    total = None
    for index in range(11):
        begin = list(starts)
        begin[axis] = index
        piece = lax.slice_in_dim(padded, begin[axis], begin[axis] + length, axis=axis)
        term = filter_weights[index] * piece
        total = term if total is None else total + term
    return total


def local(fields, strength):
    cells_x = fields.shape[1]
    cells_y = fields.shape[2]
    cells_z = fields.shape[3]
    padded_x = with_halo(fields, (("gx", 1),), 5)
    summed = difference_along(padded_x, 1, cells_x, (0, 0, 0, 0))
    padded_y = with_halo(fields, (("gy", 2),), 5)
    summed = summed + difference_along(padded_y, 2, cells_y, (0, 0, 0, 0))
    padded_z = with_halo(fields, (("gz", 3),), 5)
    summed = summed + difference_along(padded_z, 3, cells_z, (0, 0, 0, 0))
    return fields + (strength / 1024.0)[:, None, None, None] * summed


def solution(mesh):
    return jax.shard_map(
        local,
        mesh=mesh,
        in_specs=(P(None, "gx", "gy", "gz"), P()),
        out_specs=P(None, "gx", "gy", "gz"),
        check_vma=False,
    )
```

profile of v0, /device:TPU:1, one launch (start us, length us, event | category | flops | bytes accessed | tf_op | source)
XLA Modules:
  0.0 95.2 jit_solution(4387349442912395985)
XLA Ops:
  0.0 1.7 %fusion.58 = (f32[32,8,5,128]{3,2,1,0:T(8,128)S(1)}, f32[32,8,5,128]{3,2,1,0:T(8,128)S(1)}) fusion(f32[32,8,8,128]{3,2,1,0:T(8,128)} %param.2), kind=kLoop, calls=%fused_computation.105 | loop fusion | bytes 2621440 | tf_op jit(solution)/shard_map/slice | solution.py:12
  1.7 0.0 copy-start
  1.7 1.0 %copy.11 = f32[32,8,5,128]{3,1,2,0:T(8,128)} copy(f32[32,8,5,128]{3,2,1,0:T(8,128)S(1)} %get-tuple-element.11) | data formatting | bytes 1310720
  2.7 4.0 %collective-permute-start.2 = (f32[32,8,5,128]{3,1,2,0:T(8,128)}, f32[32,8,5,128]{3,1,2,0:T(8,128)}, u32[]{:S(2)}, u32[]{:S(2)}) collective-permute-start(f32[32,8,5,128]{3,1,2,0:T(8,128)} %copy.11), channel_id=1, source_target_pairs={{0,4},{4,8},{8,12},{12,16},{16,20},{20,24},{24,28},{28,0},{1,5},{5... | collective-permute-start | bytes 1966088 | tf_op jit(solution)/shard_map/ppermute | solution.py:16
  6.7 0.0 copy-done
  6.7 1.1 %fusion.57 = (f32[32,5,8,128]{3,2,1,0:T(8,128)}, f32[32,5,8,128]{3,2,1,0:T(8,128)}) fusion(f32[32,8,8,128]{3,2,1,0:T(8,128)S(1)} %copy-done), kind=kLoop, calls=%fused_computation.104 | loop fusion | bytes 2621440 | tf_op jit(solution)/shard_map/slice | solution.py:13
  7.9 11.5 %collective-permute-start = (f32[32,5,8,128]{3,2,1,0:T(8,128)}, f32[32,5,8,128]{3,2,1,0:T(8,128)}, u32[]{:S(2)}, u32[]{:S(2)}) collective-permute-start(f32[32,5,8,128]{3,2,1,0:T(8,128)} %get-tuple-element.8), channel_id=1, source_target_pairs={{0,32},{32,64},{64,96},{96,128},{128,160},{160,192},{192,224},{224... | collective-permute-start | bytes 1966088 | tf_op jit(solution)/shard_map/ppermute | solution.py:16
  19.3 1.0 %copy.12 = f32[32,8,5,128]{3,1,2,0:T(8,128)} copy(f32[32,8,5,128]{3,2,1,0:T(8,128)S(1)} %get-tuple-element.10) | data formatting | bytes 1310720
  20.4 3.5 %collective-permute-start.3 = (f32[32,8,5,128]{3,1,2,0:T(8,128)}, f32[32,8,5,128]{3,1,2,0:T(8,128)}, u32[]{:S(2)}, u32[]{:S(2)}) collective-permute-start(f32[32,8,5,128]{3,1,2,0:T(8,128)} %copy.12), channel_id=1, source_target_pairs={{4,0},{8,4},{12,8},{16,12},{20,16},{24,20},{28,24},{0,28},{5,1},{9... | collective-permute-start | bytes 1966088 | tf_op jit(solution)/shard_map/ppermute | solution.py:18
  23.9 0.4 fusion.59
  24.3 0.0 copy-start.3
  24.3 1.3 %copy.14 = f32[32,8,8,5]{0,2,3,1:T(8,128)} copy(f32[32,8,8,5]{3,2,1,0:T(8,128)S(1)} %get-tuple-element.13) | data formatting | bytes 81920
  25.6 7.3 %collective-permute-start.5 = (f32[32,8,8,5]{0,2,3,1:T(8,128)}, f32[32,8,8,5]{0,2,3,1:T(8,128)S(1)}, u32[]{:S(2)}, u32[]{:S(2)}) collective-permute-start(f32[32,8,8,5]{0,2,3,1:T(8,128)} %copy.14), channel_id=1, source_target_pairs={{1,0},{2,1},{3,2},{0,3},{5,4},{6,5},{7,6},{4,7},{9,8},{10,9},{11,1... | collective-permute-start | bytes 122888 | tf_op jit(solution)/shard_map/ppermute | solution.py:18
  32.9 1.9 %collective-permute-start.1 = (f32[32,5,8,128]{3,2,1,0:T(8,128)}, f32[32,5,8,128]{3,2,1,0:T(8,128)S(1)}, u32[]{:S(2)}, u32[]{:S(2)}) collective-permute-start(f32[32,5,8,128]{3,2,1,0:T(8,128)} %get-tuple-element.9), channel_id=1, source_target_pairs={{32,0},{64,32},{96,64},{128,96},{160,128},{192,160},{224,192},{256... | collective-permute-start | bytes 1966088 | tf_op jit(solution)/shard_map/ppermute | solution.py:18
  34.8 0.7 copy.13
  35.5 17.8 %collective-permute-done.5 = f32[32,8,8,5]{0,2,3,1:T(8,128)S(1)} collective-permute-done((f32[32,8,8,5]{0,2,3,1:T(8,128)}, f32[32,8,8,5]{0,2,3,1:T(8,128)S(1)}, u32[]{:S(2)}, u32[]{:S(2)}) %collective-permute-start.5) | collective-permute-done | bytes 40992 | tf_op jit(solution)/shard_map/ppermute | solution.py:18
  53.3 1.9 %collective-permute-start.4 = (f32[32,8,8,5]{0,2,3,1:T(8,128)S(1)}, f32[32,8,8,5]{0,2,3,1:T(8,128)S(1)}, u32[]{:S(2)}, u32[]{:S(2)}) collective-permute-start(f32[32,8,8,5]{0,2,3,1:T(8,128)S(1)} %copy.13), channel_id=1, source_target_pairs={{0,1},{1,2},{2,3},{3,0},{4,5},{5,6},{6,7},{7,4},{8,9},{9,10},{10,1... | collective-permute-start | bytes 122888 | tf_op jit(solution)/shard_map/ppermute | solution.py:16
  55.2 0.0 copy-done.3
  55.2 1.9 %copy.10 = f32[32,8,8,5]{3,2,1,0:T(8,128)} copy(f32[32,8,8,5]{0,2,3,1:T(8,128)S(1)} %collective-permute-done.5) | data formatting | bytes 81920 | tf_op jit(solution)/shard_map/ppermute | solution.py:18
  57.1 13.1 %collective-permute-done.4 = f32[32,8,8,5]{0,2,3,1:T(8,128)S(1)} collective-permute-done((f32[32,8,8,5]{0,2,3,1:T(8,128)S(1)}, f32[32,8,8,5]{0,2,3,1:T(8,128)S(1)}, u32[]{:S(2)}, u32[]{:S(2)}) %collective-permute-start.4) | collective-permute-done | bytes 40992 | tf_op jit(solution)/shard_map/ppermute | solution.py:16
  70.2 1.8 %copy.8 = f32[32,8,8,5]{3,2,1,0:T(8,128)} copy(f32[32,8,8,5]{0,2,3,1:T(8,128)S(1)} %collective-permute-done.4) | data formatting | bytes 81920 | tf_op jit(solution)/shard_map/ppermute | solution.py:16
  72.0 0.0 collective-permute-done.2
  72.0 2.3 %copy.4 = f32[32,8,5,128]{3,2,1,0:T(8,128)} copy(f32[32,8,5,128]{3,1,2,0:T(8,128)} %collective-permute-done.2) | data formatting | bytes 1310720 | tf_op jit(solution)/shard_map/ppermute | solution.py:16
  74.3 0.0 collective-permute-done
  74.3 1.1 %constant_dynamic-update-slice_fusion.1 = f32[32,13,8,128]{3,2,1,0:T(8,128)S(1)} fusion(f32[32,5,8,128]{3,2,1,0:T(8,128)} %collective-permute-done), kind=kLoop, calls=%fused_computation.99 | loop fusion | bytes 1310720
  75.4 0.2 constant_dynamic-update-slice_fusion
  75.7 0.0 copy-start.1
  75.7 0.0 collective-permute-done.3
  75.7 1.8 %copy_dynamic-update-slice_fusion = f32[32,8,13,128]{3,2,1,0:T(8,128)S(1)} fusion(f32[32,8,13,128]{3,2,1,0:T(8,128)S(1)} %get-tuple-element.7, f32[32,8,5,128]{3,1,2,0:T(8,128)} %collective-permute-done.3), kind=kLoop, calls=%fused_computation.97 | loop fusion | bytes 1703936 | tf_op jit(solution)/shard_map/concatenate | solution.py:14
  77.5 0.0 collective-permute-done.1
  77.5 1.3 %copy-done.2 = f32[32,8,13,128]{3,2,1,0:T(8,128)} copy-done((f32[32,8,13,128]{3,2,1,0:T(8,128)}, f32[32,8,13,128]{3,2,1,0:T(8,128)S(1)}, u32[]{:S(2)}) %copy-start.2) | copy-done | bytes 1703960
  78.8 16.4 %fusion.6 = f32[32,8,8,128]{3,2,1,0:T(8,128)} fusion(f32[32,8,8,128]{3,2,1,0:T(8,128)S(1)} %copy-done, f32[32,8,8,5]{3,2,1,0:T(8,128)} %copy.10, f32[32,8,8,5]{3,2,1,0:T(8,128)} %copy.8, f32[32,8,5,128]{3,2,1,0:T(8,128)} %copy.4, f32[32,8,13,128]{3,2,1,0:T(8,128)} %copy-done.2, f32[32,13,8,128]{3,2,1,0:T(8,128)S(1)} %constant_dynamic-update-slice_fusion.2, ...), kind=kLoop, calls=%fused_computation.30 | loop fusion | flops 19398656 | bytes 18563200 | tf_op jit(solution)/shard_map/add | solution.py:46
  (4 shorter events, 0.1 us)
Async XLA Ops:
  1.7 5.0 %copy-start = (f32[32,8,8,128]{3,2,1,0:T(8,128)S(1)}, f32[32,8,8,128]{3,2,1,0:T(8,128)}, u32[]{:S(2)}) copy-start(f32[32,8,8,128]{3,2,1,0:T(8,128)} %param.2) | copy-start | bytes 3145732
  2.7 69.3 %collective-permute-start.2 = (f32[32,8,5,128]{3,1,2,0:T(8,128)}, f32[32,8,5,128]{3,1,2,0:T(8,128)}, u32[]{:S(2)}, u32[]{:S(2)}) collective-permute-start(f32[32,8,5,128]{3,1,2,0:T(8,128)} %copy.11), channel_id=1, source_target_pairs={{0,4},{4,8},{8,12},{12,16},{16,20},{20,24},{24,28},{28,0},{1,5},{5... | collective-permute-start | bytes 1966088 | tf_op jit(solution)/shard_map/ppermute | solution.py:16
  7.9 66.4 %collective-permute-start = (f32[32,5,8,128]{3,2,1,0:T(8,128)}, f32[32,5,8,128]{3,2,1,0:T(8,128)}, u32[]{:S(2)}, u32[]{:S(2)}) collective-permute-start(f32[32,5,8,128]{3,2,1,0:T(8,128)} %get-tuple-element.8), channel_id=1, source_target_pairs={{0,32},{32,64},{64,96},{96,128},{128,160},{160,192},{192,224},{224... | collective-permute-start | bytes 1966088 | tf_op jit(solution)/shard_map/ppermute | solution.py:16
  20.4 55.3 %collective-permute-start.3 = (f32[32,8,5,128]{3,1,2,0:T(8,128)}, f32[32,8,5,128]{3,1,2,0:T(8,128)}, u32[]{:S(2)}, u32[]{:S(2)}) collective-permute-start(f32[32,8,5,128]{3,1,2,0:T(8,128)} %copy.12), channel_id=1, source_target_pairs={{4,0},{8,4},{12,8},{16,12},{20,16},{24,20},{28,24},{0,28},{5,1},{9... | collective-permute-start | bytes 1966088 | tf_op jit(solution)/shard_map/ppermute | solution.py:18
  24.3 30.9 %copy-start.3 = (f32[32]{0:T(128)S(1)}, f32[32]{0:T(128)}, u32[]{:S(2)}) copy-start(f32[32]{0:T(128)} %param.3) | copy-start | bytes 388
  25.6 27.7 %collective-permute-start.5 = (f32[32,8,8,5]{0,2,3,1:T(8,128)}, f32[32,8,8,5]{0,2,3,1:T(8,128)S(1)}, u32[]{:S(2)}, u32[]{:S(2)}) collective-permute-start(f32[32,8,8,5]{0,2,3,1:T(8,128)} %copy.14), channel_id=1, source_target_pairs={{1,0},{2,1},{3,2},{0,3},{5,4},{6,5},{7,6},{4,7},{9,8},{10,9},{11,1... | collective-permute-start | bytes 122888 | tf_op jit(solution)/shard_map/ppermute | solution.py:18
  32.9 44.6 %collective-permute-start.1 = (f32[32,5,8,128]{3,2,1,0:T(8,128)}, f32[32,5,8,128]{3,2,1,0:T(8,128)S(1)}, u32[]{:S(2)}, u32[]{:S(2)}) collective-permute-start(f32[32,5,8,128]{3,2,1,0:T(8,128)} %get-tuple-element.9), channel_id=1, source_target_pairs={{32,0},{64,32},{96,64},{128,96},{160,128},{192,160},{224,192},{256... | collective-permute-start | bytes 1966088 | tf_op jit(solution)/shard_map/ppermute | solution.py:18
  53.3 16.9 %collective-permute-start.4 = (f32[32,8,8,5]{0,2,3,1:T(8,128)S(1)}, f32[32,8,8,5]{0,2,3,1:T(8,128)S(1)}, u32[]{:S(2)}, u32[]{:S(2)}) collective-permute-start(f32[32,8,8,5]{0,2,3,1:T(8,128)S(1)} %copy.13), channel_id=1, source_target_pairs={{0,1},{1,2},{2,3},{3,0},{4,5},{5,6},{6,7},{7,4},{8,9},{9,10},{10,1... | collective-permute-start | bytes 122888 | tf_op jit(solution)/shard_map/ppermute | solution.py:16
  75.7 1.9 %copy-start.1 = (f32[32,13,8,128]{3,2,1,0:T(8,128)}, f32[32,13,8,128]{3,2,1,0:T(8,128)S(1)}, u32[]{:S(2)}) copy-start(f32[32,13,8,128]{3,2,1,0:T(8,128)S(1)} %get-tuple-element.5) | copy-start | bytes 5111812
  77.5 1.4 %copy-start.2 = (f32[32,8,13,128]{3,2,1,0:T(8,128)}, f32[32,8,13,128]{3,2,1,0:T(8,128)S(1)}, u32[]{:S(2)}) copy-start(f32[32,8,13,128]{3,2,1,0:T(8,128)S(1)} %copy_dynamic-update-slice_fusion) | copy-start | bytes 5111812
where the time goes:
time: 95.7 us; the launch traced here: 95.2 us
  waiting for transfers between devices  30.9 us (32%)
  starting transfers between devices  30.1 us (31%)
  local copies, waits for them, and re-layouts  17.6 us (18%)
  other arithmetic  16.4 us (17%)
    ppermute x3, waiting for transfers between devices, with_halo(): lax.ppermute(head, axis, [((i + 1) % count, i) for i in range(count)])  17.8 us
    ppermute x3, starting transfers between devices, with_halo(): lax.ppermute(tail, axis, [(i, (i + 1) % count) for i in range(count)])  17.4 us
    add x1, other arithmetic, local(): return fields + (strength / 1024.0)[:, None, None, None] * summed  16.4 us
    ppermute x3, waiting for transfers between devices, with_halo(): lax.ppermute(tail, axis, [(i, (i + 1) % count) for i in range(count)])  13.1 us
    ppermute x3, starting transfers between devices, with_halo(): lax.ppermute(head, axis, [((i + 1) % count, i) for i in range(count)])  12.8 us
    unnamed x13, local copies, waits for them, and re-layouts  6.35 us
    ppermute x2, local copies, waits for them, and re-layouts, with_halo(): lax.ppermute(tail, axis, [(i, (i + 1) % count) for i in range(count)])  4.1 us
    concatenate x3, local copies, waits for them, and re-layouts, with_halo(): jnp.concatenate([lax.ppermute(tail, axis, [(i, (i + 1) % count) for i in...  2.03 us
  transfers between devices with their start and end apart: 6, of which 2 were waited for; matrix products, arithmetic and copies ran while one was open for 14% of the time, Pallas kernels for 0%

commit v1 on v0

v1 whole, which is shorter than its diff:
```python
import functools

import jax
import jax.numpy as jnp
from jax import lax
from jax.experimental import pallas as pl
from jax.experimental.pallas import tpu as pltpu
from jax.sharding import PartitionSpec as P

MESH = pl.DeviceIdType.MESH

center = -252.0
weights = (210.0, -120.0, 45.0, -10.0, 1.0)
reach = 5

Z_GROUPS = 3
chunks = 8
relays = 3


def tap_sum(tiles, length):
    out = []
    for i in range(length):
        total = center * tiles[i + reach]
        for k in range(1, reach + 1):
            total = total + weights[k - 1] * (tiles[i + reach - k] + tiles[i + reach + k])
        out.append(total)
    return out


def kernel(
    sizes,
    fields,
    strength,
    out,
    xp,
    yt,
    acc,
    hold,
    zs,
    zr,
    scale,
    load_sem,
    scale_sem,
    x_send,
    hold_recv,
    far_recv,
    near_send,
    near_recv,
    y_send,
    y_recv,
    z_send,
    z_recv,
):
    nx, ny, nz = sizes
    species = xp.shape[0]
    cells = fields.shape[1]
    per = species // chunks
    pairs = species // 2

    gx = lax.axis_index("gx")
    gy = lax.axis_index("gy")
    gz = lax.axis_index("gz")
    core = lax.rem(gx, 2)
    chip = lax.div(gx, 2)
    z_hi = lax.rem(chip, Z_GROUPS)
    chip_x = lax.div(chip, Z_GROUPS)
    x_count = nx // (2 * Z_GROUPS)
    z_count = Z_GROUPS * nz
    z = z_hi * nz + gz
    step = 2 * core - 1

    def place(at_x, at_z, at_core):
        at_z = lax.rem(at_z + 2 * z_count, z_count)
        at_x = lax.rem(at_x + x_count, x_count)
        hi = lax.div(at_z, nz)
        return {"gx": (at_x * Z_GROUPS + hi) * 2 + at_core, "gz": lax.rem(at_z, nz)}

    edge = jnp.where(core == 1, Z_GROUPS - 1, 0)
    relay_to = place(chip_x, z + step, core)
    relay_from = place(chip_x, z - step, core)
    origin = lax.div(lax.rem(z - 3 * step + 2 * z_count, z_count), nz)
    last_to = place(jnp.where(origin == edge, chip_x + step, chip_x), z + step, 1 - core)
    back = -step
    before = lax.div(lax.rem(z - 4 * back + 2 * z_count, z_count), nz)
    back_edge = jnp.where(core == 1, 0, Z_GROUPS - 1)
    last_from = place(jnp.where(before == back_edge, chip_x - back, chip_x), z - back, 1 - core)
    partner = {"gx": chip * 2 + 1 - core}
    y_up = {"gy": lax.rem(gy + 1, ny)}
    y_down = {"gy": lax.rem(gy + ny - 1, ny)}
    z_up = {"gz": lax.rem(gz + 1, nz)}
    z_down = {"gz": lax.rem(gz + nz - 1, nz)}

    barrier = pltpu.get_barrier_semaphore()
    for who in (relay_from, last_from, partner, y_up, y_down, z_up, z_down):
        pl.semaphore_signal(barrier, inc=1, device_id=who, device_id_type=MESH)

    def load(j):
        return pltpu.make_async_copy(
            fields.at[pl.ds(j * per, per)], xp.at[pl.ds(j * per, per), pl.ds(reach, cells)], load_sem.at[j]
        )

    for j in range(chunks):
        load(j).start()
    scale_copy = pltpu.make_async_copy(strength, scale, scale_sem)
    scale_copy.start()
    for j in range(chunks):
        load(j).wait()

    def pack(p, _):
        block = xp[pl.ds(2 * p, 2), pl.ds(reach, cells)].reshape(128, 128)
        turned = jnp.transpose(block)
        zs[0, p] = turned[0:8]
        zs[1, p] = turned[120:128]
        return 0

    lax.fori_loop(0, pairs, pack, 0)

    pl.semaphore_wait(barrier, 7)

    away = reach + (cells - reach) * core
    arrive = (reach + cells) * (1 - core)

    def first_hop(j):
        return pltpu.make_async_remote_copy(
            src_ref=xp.at[pl.ds(j * per, per), pl.ds(away, reach)],
            dst_ref=hold.at[0, pl.ds(j * per, per)],
            send_sem=x_send.at[0, j],
            recv_sem=hold_recv.at[0, j],
            device_id=relay_to,
            device_id_type=MESH,
        )

    def mid_hop(h, j):
        return pltpu.make_async_remote_copy(
            src_ref=hold.at[h - 1, pl.ds(j * per, per)],
            dst_ref=hold.at[h, pl.ds(j * per, per)],
            send_sem=x_send.at[h, j],
            recv_sem=hold_recv.at[h, j],
            device_id=relay_to,
            device_id_type=MESH,
        )

    def last_hop(j):
        return pltpu.make_async_remote_copy(
            src_ref=hold.at[relays - 1, pl.ds(j * per, per)],
            dst_ref=xp.at[pl.ds(j * per, per), pl.ds((reach + cells) * (1 - core), reach)],
            send_sem=x_send.at[relays, j],
            recv_sem=far_recv.at[j],
            device_id=last_to,
            device_id_type=MESH,
        )

    def last_hop_in(j):
        return pltpu.make_async_remote_copy(
            src_ref=hold.at[relays - 1, pl.ds(j * per, per)],
            dst_ref=xp.at[pl.ds(j * per, per), pl.ds((reach + cells) * core, reach)],
            send_sem=x_send.at[relays, j],
            recv_sem=far_recv.at[j],
            device_id=last_to,
            device_id_type=MESH,
        )

    near = pltpu.make_async_remote_copy(
        src_ref=xp.at[:, pl.ds(reach + (cells - reach) * (1 - core), reach)],
        dst_ref=xp.at[:, pl.ds((reach + cells) * core, reach)],
        send_sem=near_send,
        recv_sem=near_recv,
        device_id=partner,
        device_id_type=MESH,
    )

    def z_copy(side, to):
        return pltpu.make_async_remote_copy(
            src_ref=zs.at[side],
            dst_ref=zr.at[side],
            send_sem=z_send.at[side],
            recv_sem=z_recv.at[side],
            device_id=to,
            device_id_type=MESH,
        )

    y_first = pltpu.make_async_remote_copy(
        src_ref=yt.at[:, pl.ds(reach, reach)],
        dst_ref=yt.at[:, pl.ds(reach + cells, reach)],
        send_sem=y_send.at[0],
        recv_sem=y_recv.at[0],
        device_id=y_down,
        device_id_type=MESH,
    )
    y_last = pltpu.make_async_remote_copy(
        src_ref=yt.at[:, pl.ds(cells, reach)],
        dst_ref=yt.at[:, pl.ds(0, reach)],
        send_sem=y_send.at[1],
        recv_sem=y_recv.at[1],
        device_id=y_up,
        device_id_type=MESH,
    )

    for j in range(chunks):
        first_hop(j).start()
    z_low = z_copy(0, z_down)
    z_high = z_copy(1, z_up)
    z_low.start()
    z_high.start()
    near.start()

    def turn(s, _):
        yt[s, pl.ds(reach, cells)] = jnp.swapaxes(xp[s, pl.ds(reach, cells)], 0, 1)
        return 0

    lax.fori_loop(0, species, turn, 0)
    y_first.start()
    y_last.start()

    z_low.wait()
    z_high.wait()
    lane = lax.broadcasted_iota(jnp.int32, (8, 128), 1)

    def z_sum(p, _):
        edges = jnp.concatenate([zr[0, p], jnp.zeros((112, 128), jnp.float32), zr[1, p]], axis=0)
        beside = jnp.transpose(edges)
        for half in range(2):
            for x in range(8):
                row = half * 8 + x
                own = xp[2 * p + half, reach + x]
                other = beside[row * 8 : row * 8 + 8]
                total = center * own
                for k in range(1, reach + 1):
                    left = pltpu.roll(jnp.where(lane >= 128 - k, other, own), k, 1)
                    right = pltpu.roll(jnp.where(lane < k, other, own), 128 - k, 1)
                    total = total + weights[k - 1] * (left + right)
                acc[2 * p + half, x] = total
        return 0

    lax.fori_loop(0, pairs, z_sum, 0)

    for j in range(chunks):
        first_hop(j).wait_recv()
        mid_hop(1, j).start()

    for j in range(chunks):
        mid_hop(1, j).wait_recv()
        mid_hop(2, j).start()

    y_first.wait()
    y_last.wait()

    def y_sum(s, _):
        tiles = [yt[s, i] for i in range(cells + 2 * reach)]
        total = jnp.stack(tap_sum(tiles, cells), axis=0)
        acc[s] = acc[s] + jnp.swapaxes(total, 0, 1)
        return 0

    lax.fori_loop(0, species, y_sum, 0)

    for j in range(chunks):
        mid_hop(2, j).wait_recv()
        last_hop(j).start()

    near.wait()
    scale_copy.wait()

    for j in range(chunks):
        last_hop_in(j).wait_recv()

        def finish(i, _):
            s = j * per + i
            tiles = [xp[s, i] for i in range(cells + 2 * reach)]
            total = tap_sum(tiles, cells)
            factor = scale[s] * (1.0 / 1024.0)
            for x in range(cells):
                out[s, x] = tiles[reach + x] + factor * (total[x] + acc[s, x])
            return 0

        lax.fori_loop(0, per, finish, 0)

    for j in range(chunks):
        first_hop(j).wait_send()
        mid_hop(1, j).wait_send()
        mid_hop(2, j).wait_send()
        last_hop(j).wait_send()


def local(sizes, fields, strength):
    species, cells, rows, lanes = fields.shape
    return pl.pallas_call(
        functools.partial(kernel, sizes),
        out_shape=jax.ShapeDtypeStruct(fields.shape, fields.dtype),
        in_specs=[pl.BlockSpec(memory_space=pl.ANY), pl.BlockSpec(memory_space=pl.ANY)],
        out_specs=pl.BlockSpec(memory_space=pltpu.VMEM),
        scratch_shapes=[
            pltpu.VMEM((species, cells + 2 * reach, rows, lanes), jnp.float32),
            pltpu.VMEM((species, rows + 2 * reach, cells, lanes), jnp.float32),
            pltpu.VMEM((species, cells, rows, lanes), jnp.float32),
            pltpu.VMEM((relays, species, reach, rows, lanes), jnp.float32),
            pltpu.VMEM((2, species // 2, 8, 128), jnp.float32),
            pltpu.VMEM((2, species // 2, 8, 128), jnp.float32),
            pltpu.SMEM((species,), jnp.float32),
            pltpu.SemaphoreType.DMA((chunks,)),
            pltpu.SemaphoreType.DMA,
            pltpu.SemaphoreType.DMA((relays + 1, chunks)),
            pltpu.SemaphoreType.DMA((relays, chunks)),
            pltpu.SemaphoreType.DMA((chunks,)),
            pltpu.SemaphoreType.DMA,
            pltpu.SemaphoreType.DMA,
            pltpu.SemaphoreType.DMA((2,)),
            pltpu.SemaphoreType.DMA((2,)),
            pltpu.SemaphoreType.DMA((2,)),
            pltpu.SemaphoreType.DMA((2,)),
        ],
        compiler_params=pltpu.CompilerParams(collective_id=0, has_side_effects=True),
    )(fields, strength)


def solution(mesh):
    sizes = (mesh.shape["gx"], mesh.shape["gy"], mesh.shape["gz"])
    return jax.shard_map(
        functools.partial(local, sizes),
        mesh=mesh,
        in_specs=(P(None, "gx", "gy", "gz"), P()),
        out_specs=P(None, "gx", "gy", "gz"),
        check_vma=False,
    )
```

time: 95.7 us -> 61.4 us (0.64)
  the two profiles are of different devices: /device:TPU:1 before, /device:TPU:40 now
where the time goes in v1:
time: 61.4 us; the launch traced here: 61.2 us
  Pallas kernels  58.9 us (96%)
  local copies, waits for them, and re-layouts  2.31 us (4%)
    pallas_call x1, Pallas kernels, local(): pl.pallas_call(functools.partial(kernel, sizes), out_shape=jax.ShapeDtype...  58.9 us
    unnamed x1, local copies, waits for them, and re-layouts  2.31 us

profile of v1, /device:TPU:40, one launch (start us, length us, event | category | flops | bytes accessed | tf_op | source)
XLA Modules:
  0.0 61.2 jit_solution(16526484635193680638)
XLA Ops:
  0.0 58.9 %shard_map.28 = f32[32,8,8,128]{3,2,1,0:T(8,128)} custom-call(f32[32,8,8,128]{3,2,1,0:T(8,128)} %fields.1, f32[32]{0:T(128)} %strength.1), custom_call_target="tpu_custom_call" | custom-call | tf_op jit(solution)/shard_map/pallas_call | solution.py:287
  58.9 2.3 %copy.4 = f32[32,8,8,128]{3,2,1,0:T(8,128)} copy(f32[32,8,8,128]{3,2,1,0:T(8,128)} %shard_map.28) | data formatting | bytes 2097152

commit v2 on v0

v2 whole, which is shorter than its diff:
```python
import functools

import jax
import jax.numpy as jnp
from jax import lax
from jax.experimental import pallas as pl
from jax.experimental.pallas import tpu as pltpu
from jax.sharding import PartitionSpec as P

MESH = pl.DeviceIdType.MESH

center = -252.0
weights = (210.0, -120.0, 45.0, -10.0, 1.0)
reach = 5

Z_GROUPS = 3
chunks = 8
relays = 3
detour = 1


def tap_sum(tiles, length):
    out = []
    for i in range(length):
        total = center * tiles[i + reach]
        for k in range(1, reach + 1):
            total = total + weights[k - 1] * (tiles[i + reach - k] + tiles[i + reach + k])
        out.append(total)
    return out


def kernel(
    sizes,
    fields,
    strength,
    out,
    xp,
    yt,
    zt,
    acc,
    hold,
    edge,
    beside,
    round_z,
    scale,
    load_sem,
    scale_sem,
    x_send,
    detour_send,
    hold_recv,
    detour_recv,
    far_recv,
    near_send,
    near_recv,
    y_send,
    y_recv,
    z_send,
    z_recv,
    round_recv,
    round_go,
):
    nx, ny, nz = sizes
    species = xp.shape[0]
    cells = fields.shape[1]
    per = species // chunks
    pairs = species // 2
    x_count = nx // (2 * Z_GROUPS)
    first = 2 * per

    gx = lax.axis_index("gx")
    gy = lax.axis_index("gy")
    gz = lax.axis_index("gz")

    chip = lax.div(gx, 2)
    core = gx - 2 * chip
    chip_x = lax.div(chip, Z_GROUPS)
    z_hi = chip - Z_GROUPS * chip_x
    upward = core == 1
    downward = core == 0
    step = 2 * core - 1

    def wrap(v, n):
        return jnp.where(v < 0, v + n, jnp.where(v >= n, v - n, v))

    def along(d):
        lo = gz + d
        carry = jnp.where(lo < 0, -1, jnp.where(lo >= nz, 1, 0))
        return wrap(z_hi + carry, Z_GROUPS), lo - carry * nz

    def place(at_x, hi, lo, at_core):
        return {"gx": (at_x * Z_GROUPS + hi) * 2 + at_core, "gz": lo}

    ahead = along(step)
    behind = along(-step)
    crosses = jnp.where(upward, ahead[0] == 0, ahead[0] == Z_GROUPS - 1)
    relay_to = place(chip_x, *ahead, core)
    relay_from = place(chip_x, *behind, core)
    last_to = place(wrap(chip_x + jnp.where(crosses, step, 0), x_count), *ahead, 1 - core)
    crossed = jnp.where(upward, z_hi == Z_GROUPS - 1, z_hi == 0)
    last_from = place(wrap(chip_x + jnp.where(crossed, step, 0), x_count), *ahead, 1 - core)
    partner = {"gx": chip * 2 + 1 - core}
    y_up = {"gy": wrap(gy + 1, ny)}
    y_down = {"gy": wrap(gy - 1, ny)}
    z_up = {"gz": wrap(gz + 1, nz)}
    z_down = {"gz": wrap(gz - 1, nz)}
    has_up = gz < nz - 1
    has_down = gz > 0
    near_ahead = jnp.where(upward, gz < nz - 1, gz > 0)
    near_behind = jnp.where(upward, gz > 0, gz < nz - 1)

    bottom, middle, top = 0, Z_GROUPS - 2, Z_GROUPS - 1
    round_from = jnp.where(upward, top, bottom)
    round_to = top - round_from
    sends_round = z_hi == round_from
    turns_round = z_hi == middle
    beyond = wrap(chip_x + step, x_count) * Z_GROUPS
    round_mid = {"gx": (chip_x * Z_GROUPS + middle) * 2 + core}
    round_source = {"gx": (chip_x * Z_GROUPS + round_from) * 2 + core}
    round_end = {"gx": (beyond + round_to) * 2 + 1 - core}
    round_turn = {"gx": (beyond + middle) * 2 + 1 - core}

    def skips(h):
        below = jnp.where(gz < h, wrap(z_hi - 1, Z_GROUPS), z_hi)
        above = jnp.where(gz + h >= nz, wrap(z_hi + 1, Z_GROUPS), z_hi)
        return jnp.where(upward, below, above) == round_from

    barrier = pltpu.get_barrier_semaphore()

    def greet(who):
        pl.semaphore_signal(barrier, inc=1, device_id=who, device_id_type=MESH)

    for who in (relay_from, last_from, partner, y_up, y_down):
        greet(who)

    @pl.when(near_ahead)
    def _():
        greet(relay_to)

    @pl.when(upward & turns_round)
    def _():
        greet(round_source)

    @pl.when(downward & turns_round)
    def _():
        greet(round_end)

    @pl.when(downward & sends_round)
    def _():
        greet(round_mid)
        greet(round_turn)

    greeted = 5 + jnp.where(near_behind, 1, 0) + jnp.where(turns_round, 1, jnp.where(upward & sends_round, 2, 0))

    loads = [
        pltpu.make_async_copy(fields.at[pl.ds(at, n)], xp.at[pl.ds(at, n), pl.ds(reach, cells)], load_sem.at[i])
        for i, (at, n) in enumerate(((0, first), (first, species - first)))
    ]
    for copy in loads:
        copy.start()
    scale_copy = pltpu.make_async_copy(strength, scale, scale_sem)
    scale_copy.start()

    def part(j):
        return pl.ds(j * per, per)

    def remote(src, dst, send, recv, to):
        return pltpu.make_async_remote_copy(
            src_ref=src, dst_ref=dst, send_sem=send, recv_sem=recv, device_id=to, device_id_type=MESH
        )

    far_there = (reach + cells) * (1 - core)
    far_here = (reach + cells) * core

    def away(j):
        return xp.at[part(j), pl.ds(reach + (cells - reach) * core, reach)]

    def hop(h, j):
        src = away(j) if h == 0 else hold.at[h - 1, part(j)]
        send = detour_send.at[h] if j < detour else x_send
        if h < relays:
            return remote(src, hold.at[h, part(j)], send, hold_recv.at[h, j], relay_to)
        return remote(src, xp.at[part(j), pl.ds(far_there, reach)], send, far_recv.at[j], last_to)

    def arrival(j):
        return remote(hold.at[0, part(j)], xp.at[part(j), pl.ds(far_here, reach)], x_send, far_recv.at[j], last_to)

    around = pl.ds(0, detour * per)

    def round_first():
        src = xp.at[around, pl.ds(reach + (cells - reach) * core, reach)]
        return remote(src, hold.at[relays, around], detour_send.at[0], detour_recv, round_mid)

    def round_last():
        dst = xp.at[around, pl.ds(far_there, reach)]
        return remote(hold.at[relays, around], dst, detour_send.at[relays + 1], far_recv.at[0], round_end)

    near = remote(
        xp.at[:, pl.ds(reach + (cells - reach) * (1 - core), reach)],
        xp.at[:, pl.ds(far_here, reach)],
        near_send,
        near_recv,
        partner,
    )
    y_copies = (
        remote(yt.at[:, pl.ds(reach, reach)], yt.at[:, pl.ds(reach + cells, reach)], y_send, y_recv, y_down),
        remote(yt.at[:, pl.ds(cells, reach)], yt.at[:, pl.ds(0, reach)], y_send, y_recv, y_up),
    )
    y_both = remote(yt.at[:, pl.ds(0, 2 * reach)], yt.at[:, pl.ds(0, 2 * reach)], y_send, y_recv, y_up)

    z_first, z_last = edge.at[0], edge.at[1]
    z_before, z_after = beside.at[0], beside.at[1]
    z_both = remote(beside, beside, z_send.at[0], z_recv, z_up)
    z_sent = [remote(edge, edge, z_send.at[i], z_recv, z_up) for i in range(2)]

    def go_up(src, dst, recv):
        return remote(src, dst, z_send.at[0], recv, z_up)

    def go_down(src, dst, recv):
        return remote(src, dst, z_send.at[1], recv, z_down)

    def z_start():
        @pl.when(has_up)
        def _():
            go_up(z_last, z_before, z_recv).start()

        @pl.when(has_down)
        def _():
            go_down(z_first, z_after, z_recv).start()

        @pl.when(gz == 0)
        def _():
            go_up(z_first, round_z.at[1], round_recv.at[1]).start()

        @pl.when(gz == nz - 1)
        def _():
            go_down(z_last, round_z.at[0], round_recv.at[0]).start()

    def z_pass():
        @pl.when(gz == 1)
        def _():
            go_up(round_z.at[1], round_z.at[1], round_recv.at[1]).wait_recv()
            go_up(round_z.at[1], round_z.at[1], round_recv.at[1]).start()

        @pl.when(gz == 2)
        def _():
            go_down(round_z.at[0], round_z.at[0], round_recv.at[0]).wait_recv()
            go_down(round_z.at[0], round_z.at[0], round_recv.at[0]).start()

    def z_pass_on():
        @pl.when(gz == 1)
        def _():
            go_down(round_z.at[0], round_z.at[0], round_recv.at[0]).wait_recv()
            go_down(round_z.at[0], z_before, z_recv).start()

        @pl.when(gz == 2)
        def _():
            go_up(round_z.at[1], round_z.at[1], round_recv.at[1]).wait_recv()
            go_up(round_z.at[1], z_after, z_recv).start()

    def z_turn(p, _):
        turned = jnp.transpose(xp[pl.ds(2 * p, 2), pl.ds(reach, cells)].reshape(128, 128))
        zt[p, 8:136] = turned
        for i in range(reach):
            edge[0, i, pl.ds(p, 1)] = turned[i : i + 1]
            edge[1, i, pl.ds(p, 1)] = turned[128 - reach + i : 129 - reach + i]
        return 0

    def y_turn(s, _):
        yt[s, pl.ds(reach, cells)] = jnp.swapaxes(xp[s, pl.ds(reach, cells)], 0, 1)
        return 0

    def z_sum(p, _):
        for i in range(reach):
            zt[p, 8 - reach + i : 9 - reach + i] = beside[0, i, pl.ds(p, 1)]
            zt[p, 136 + i : 137 + i] = beside[1, i, pl.ds(p, 1)]
        rows = []
        for r in range(16):
            at = 8 + 8 * r
            total = center * zt[p, at : at + 8]
            for k in range(1, reach + 1):
                total = total + weights[k - 1] * (zt[p, at - k : at - k + 8] + zt[p, at + k : at + k + 8])
            rows.append(total)
        acc[pl.ds(2 * p, 2)] = jnp.transpose(jnp.concatenate(rows, axis=0)).reshape(2, 8, 8, 128)
        return 0

    def y_sum(s, _):
        tiles = [yt[s, i] for i in range(cells + 2 * reach)]
        acc[s] = acc[s] + jnp.swapaxes(jnp.stack(tap_sum(tiles, cells), axis=0), 0, 1)
        return 0

    def finish(s, _):
        tiles = [xp[s, i] for i in range(cells + 2 * reach)]
        total = tap_sum(tiles, cells)
        factor = scale[s] * (1.0 / 1024.0)
        for x in range(cells):
            out[s, x] = tiles[reach + x] + factor * (total[x] + acc[s, x])
        return 0

    def relay(h):
        for j in range(chunks):
            if j < detour:

                @pl.when(jnp.logical_not(skips(h)))
                def _(j=j):
                    hop(h - 1, j).wait_recv()
                    hop(h, j).start()

            else:
                hop(h - 1, j).wait_recv()
                hop(h, j).start()

    with jax.named_scope("load_first"):
        loads[0].wait()
    with jax.named_scope("barrier_wait"):
        pl.semaphore_wait(barrier, greeted)

    @pl.when(downward & turns_round)
    def _():
        pl.semaphore_signal(round_go, inc=1, device_id=round_source, device_id_type=MESH)

    @pl.when(upward & sends_round)
    def _():
        pl.semaphore_signal(round_go, inc=1, device_id=round_turn, device_id_type=MESH)
        round_first().start()

    @pl.when(jnp.logical_not(sends_round))
    def _():
        for j in range(detour):
            hop(0, j).start()

    hop(0, 1).start()
    with jax.named_scope("load_rest"):
        loads[1].wait()
    hop(0, 2).start()
    with jax.named_scope("z_turn"):
        lax.fori_loop(0, pairs, z_turn, 0, unroll=2)
    with jax.named_scope("y_turn"):
        lax.fori_loop(0, species, y_turn, 0, unroll=2)
    with jax.named_scope("starts"):
        near.start()
        z_start()
        for j in range(3, chunks):
            hop(0, j).start()
        for copy in y_copies:
            copy.start()
    with jax.named_scope("relay1"):
        relay(1)
    with jax.named_scope("z_pass"):
        z_pass()
    with jax.named_scope("round_first"):

        @pl.when(downward & sends_round)
        def _():
            pl.semaphore_wait(round_go, 1)
            round_first().start()

    with jax.named_scope("relay2"):
        relay(2)
    with jax.named_scope("round_turn"):

        @pl.when(downward & turns_round)
        def _():
            pl.semaphore_wait(round_go, 1)

        @pl.when(turns_round)
        def _():
            round_first().wait_recv()
            round_last().start()

    with jax.named_scope("z_pass_on"):
        z_pass_on()
    with jax.named_scope("relay3"):
        relay(3)
    with jax.named_scope("z_wait"):
        z_both.wait_recv()
    with jax.named_scope("z_sum"):
        lax.fori_loop(0, pairs, z_sum, 0)
    with jax.named_scope("y_wait"):
        y_both.wait_recv()
    with jax.named_scope("y_sum"):
        lax.fori_loop(0, species, y_sum, 0)
    with jax.named_scope("near_wait"):
        near.wait()
        scale_copy.wait()
    with jax.named_scope("sent_wait"):
        y_both.wait_send()

        @pl.when(has_up)
        def _():
            z_sent[0].wait_send()

        @pl.when(has_down)
        def _():
            z_sent[1].wait_send()

    with jax.named_scope("finish"):
        for j in range(chunks):
            arrival(j).wait_recv()
            lax.fori_loop(j * per, (j + 1) * per, finish, 0)
    with jax.named_scope("send_wait"):
        hop(0, 0).wait_send()
        for h in range(1, relays + 1):

            @pl.when(jnp.logical_not(skips(h)))
            def _(h=h):
                hop(h, 0).wait_send()

        @pl.when(turns_round)
        def _():
            round_last().wait_send()

        rest = hold.at[:, pl.ds(detour * per, species - detour * per)]
        remote(rest, rest, x_send, far_recv.at[0], relay_to).wait_send()


def local(sizes, fields, strength):
    species, cells, rows, lanes = fields.shape
    return pl.pallas_call(
        functools.partial(kernel, sizes),
        out_shape=pltpu.VMEM(fields.shape, fields.dtype),
        in_specs=[pl.BlockSpec(memory_space=pl.ANY), pl.BlockSpec(memory_space=pl.ANY)],
        out_specs=pl.BlockSpec(memory_space=pltpu.VMEM),
        scratch_shapes=[
            pltpu.VMEM((species, cells + 2 * reach, rows, lanes), jnp.float32),
            pltpu.VMEM((species, rows + 2 * reach, cells, lanes), jnp.float32),
            pltpu.VMEM((species // 2, lanes + 16, 128), jnp.float32),
            pltpu.VMEM((species, cells, rows, lanes), jnp.float32),
            pltpu.VMEM((relays + 1, species, reach, rows, lanes), jnp.float32),
            pltpu.VMEM((2, reach, species // 2, 128), jnp.float32),
            pltpu.VMEM((2, reach, species // 2, 128), jnp.float32),
            pltpu.VMEM((2, reach, species // 2, 128), jnp.float32),
            pltpu.SMEM((species,), jnp.float32),
            pltpu.SemaphoreType.DMA((2,)),
            pltpu.SemaphoreType.DMA,
            pltpu.SemaphoreType.DMA,
            pltpu.SemaphoreType.DMA((relays + 2,)),
            pltpu.SemaphoreType.DMA((relays, chunks)),
            pltpu.SemaphoreType.DMA,
            pltpu.SemaphoreType.DMA((chunks,)),
            pltpu.SemaphoreType.DMA,
            pltpu.SemaphoreType.DMA,
            pltpu.SemaphoreType.DMA,
            pltpu.SemaphoreType.DMA,
            pltpu.SemaphoreType.DMA((2,)),
            pltpu.SemaphoreType.DMA,
            pltpu.SemaphoreType.DMA((2,)),
            pltpu.SemaphoreType.REGULAR,
        ],
        compiler_params=pltpu.CompilerParams(collective_id=0, has_side_effects=True),
    )(fields, strength)


def solution(mesh):
    sizes = (mesh.shape["gx"], mesh.shape["gy"], mesh.shape["gz"])
    return jax.shard_map(
        functools.partial(local, sizes),
        mesh=mesh,
        in_specs=(P(None, "gx", "gy", "gz"), P()),
        out_specs=P(None, "gx", "gy", "gz"),
        check_vma=False,
    )
```

time: 95.7 us -> 45.2 us (0.47)
  the two profiles are of different devices: /device:TPU:1 before, /device:TPU:193 now
where the time goes in v2:
time: 45.2 us; the launch traced here: 45 us
  Pallas kernels  44 us (97%)
  local copies, waits for them, and re-layouts  0.97 us (2%)
    pallas_call x1, Pallas kernels, local(): pl.pallas_call(functools.partial(kernel, sizes), out_shape=pltpu.VMEM(fie...  44 us
    unnamed x1, local copies, waits for them, and re-layouts  0.97 us

profile of v2, /device:TPU:193, one launch (start us, length us, event | category | flops | bytes accessed | tf_op | source)
XLA Modules:
  0.0 45.0 jit_solution(12708762669511687432)
XLA Ops:
  0.0 44.0 %shard_map.28 = f32[32,8,8,128]{3,2,1,0:T(8,128)S(1)} custom-call(f32[32,8,8,128]{3,2,1,0:T(8,128)} %fields.1, f32[32]{0:T(128)} %strength.1), custom_call_target="tpu_custom_call" | custom-call | tf_op jit(solution)/shard_map/pallas_call | solution.py:418
  44.0 1.0 %copy.4 = f32[32,8,8,128]{3,2,1,0:T(8,128)} copy(f32[32,8,8,128]{3,2,1,0:T(8,128)S(1)} %shard_map.28) | data formatting | bytes 2097152

commit v3 on v2

--- a/solution.py
+++ b/solution.py
@@ -14,7 +14,9 @@
 reach = 5
 
 Z_GROUPS = 3
-chunks = 8
+sizes_of_chunks = (4, 4, 4, 4, 4, 4, 4, 4)
+chunks = len(sizes_of_chunks)
+late = 3
 relays = 3
 detour = 1
 
@@ -47,6 +49,7 @@
     scale_sem,
     x_send,
     detour_send,
+    late_send,
     hold_recv,
     detour_recv,
     far_recv,
@@ -57,19 +60,27 @@
     z_send,
     z_recv,
     round_recv,
-    round_go,
+    goes,
 ):
     nx, ny, nz = sizes
     species = xp.shape[0]
     cells = fields.shape[1]
-    per = species // chunks
+    assert sum(sizes_of_chunks) == species
+    at_chunk = [sum(sizes_of_chunks[:j]) for j in range(chunks + 1)]
     pairs = species // 2
     x_count = nx // (2 * Z_GROUPS)
-    first = 2 * per
+    first = at_chunk[2]
 
     gx = lax.axis_index("gx")
     gy = lax.axis_index("gy")
     gz = lax.axis_index("gz")
+
+    loads = [
+        pltpu.make_async_copy(fields.at[pl.ds(at, n)], xp.at[pl.ds(at, n), pl.ds(reach, cells)], load_sem.at[i])
+        for i, (at, n) in enumerate(((0, first), (first, species - first)))
+    ]
+    for copy in loads:
+        copy.start()
 
     chip = lax.div(gx, 2)
     core = gx - 2 * chip
@@ -118,21 +129,42 @@
     round_source = {"gx": (chip_x * Z_GROUPS + round_from) * 2 + core}
     round_end = {"gx": (beyond + round_to) * 2 + 1 - core}
     round_turn = {"gx": (beyond + middle) * 2 + 1 - core}
+    round_ask = {"gx": (chip_x * Z_GROUPS + middle) * 2 + 1 - core}
+    round_help = {"gx": (beyond + round_to) * 2 + core}
+    round_tell = {"gx": (wrap(chip_x - step, x_count) * Z_GROUPS + middle) * 2 + core}
+    round_tell_source = {"gx": (chip_x * Z_GROUPS + bottom) * 2 + 1 - core}
+    gives_go = downward & (z_hi == top)
 
     def skips(h):
         below = jnp.where(gz < h, wrap(z_hi - 1, Z_GROUPS), z_hi)
         above = jnp.where(gz + h >= nz, wrap(z_hi + 1, Z_GROUPS), z_hi)
         return jnp.where(upward, below, above) == round_from
 
+    sends_straight = upward & (z_hi == top) & (gz == nz - 1)
+    gets_straight = downward & (z_hi == bottom) & (gz == nz - 1)
+    straight_to = {"gx": (beyond + round_to) * 2 + 1 - core}
+    straight_from = {"gx": (beyond + top) * 2 + 1 - core}
+
+    def misses(h):
+        return upward & (z_hi == bottom) & (gz == h - 1)
+
     barrier = pltpu.get_barrier_semaphore()
 
     def greet(who):
         pl.semaphore_signal(barrier, inc=1, device_id=who, device_id_type=MESH)
 
-    for who in (relay_from, last_from, partner, y_up, y_down):
+    for who in (relay_from, last_from, partner):
         greet(who)
 
-    @pl.when(near_ahead)
+    @pl.when(gy < ny - 1)
+    def _():
+        greet(y_up)
+
+    @pl.when(gy == 0)
+    def _():
+        greet(y_down)
+
+    @pl.when(upward & near_ahead)
     def _():
         greet(relay_to)
 
@@ -142,26 +174,25 @@
 
     @pl.when(downward & turns_round)
     def _():
-        greet(round_end)
+        greet(round_help)
 
     @pl.when(downward & sends_round)
     def _():
-        greet(round_mid)
+        greet(round_ask)
         greet(round_turn)
 
-    greeted = 5 + jnp.where(near_behind, 1, 0) + jnp.where(turns_round, 1, jnp.where(upward & sends_round, 2, 0))
-
-    loads = [
-        pltpu.make_async_copy(fields.at[pl.ds(at, n)], xp.at[pl.ds(at, n), pl.ds(reach, cells)], load_sem.at[i])
-        for i, (at, n) in enumerate(((0, first), (first, species - first)))
-    ]
-    for copy in loads:
-        copy.start()
+    @pl.when(gets_straight)
+    def _():
+        greet(straight_from)
+
+    also = jnp.where(sends_straight, 1, 0) + jnp.where(upward & near_behind, 1, 0) + jnp.where(gy == ny - 1, 2, jnp.where(gy > 0, 1, 0))
+    greeted = 3 + also + jnp.where(upward & turns_round, 2, jnp.where(gives_go | (upward & sends_round), 1, 0))
+
     scale_copy = pltpu.make_async_copy(strength, scale, scale_sem)
     scale_copy.start()
 
     def part(j):
-        return pl.ds(j * per, per)
+        return pl.ds(at_chunk[j], sizes_of_chunks[j])
 
     def remote(src, dst, send, recv, to):
         return pltpu.make_async_remote_copy(
@@ -176,7 +207,7 @@
 
     def hop(h, j):
         src = away(j) if h == 0 else hold.at[h - 1, part(j)]
-        send = detour_send.at[h] if j < detour else x_send
+        send = detour_send.at[h] if j < detour else late_send.at[h] if j >= chunks - late else x_send
         if h < relays:
             return remote(src, hold.at[h, part(j)], send, hold_recv.at[h, j], relay_to)
         return remote(src, xp.at[part(j), pl.ds(far_there, reach)], send, far_recv.at[j], last_to)
@@ -184,7 +215,11 @@
     def arrival(j):
         return remote(hold.at[0, part(j)], xp.at[part(j), pl.ds(far_here, reach)], x_send, far_recv.at[j], last_to)
 
-    around = pl.ds(0, detour * per)
+    def straight(j):
+        dst = xp.at[part(j), pl.ds(far_there, reach)]
+        return remote(away(j), dst, late_send.at[0], far_recv.at[j], straight_to)
+
+    around = part(0)
 
     def round_first():
         src = xp.at[around, pl.ds(reach + (cells - reach) * core, reach)]
@@ -219,6 +254,10 @@
         return remote(src, dst, z_send.at[1], recv, z_down)
 
     def z_start():
+        @pl.when(downward & has_up)
+        def _():
+            pl.semaphore_wait(goes.at[1], 1)
+
         @pl.when(has_up)
         def _():
             go_up(z_last, z_before, z_recv).start()
@@ -305,7 +344,13 @@
                     hop(h - 1, j).wait_recv()
                     hop(h, j).start()
 
-            else:
+            elif j < chunks - late:
+                hop(h - 1, j).wait_recv()
+                hop(h, j).start()
+
+        @pl.when(jnp.logical_not(misses(h)))
+        def _():
+            for j in range(chunks - late, chunks):
                 hop(h - 1, j).wait_recv()
                 hop(h, j).start()
 
@@ -314,13 +359,8 @@
     with jax.named_scope("barrier_wait"):
         pl.semaphore_wait(barrier, greeted)
 
-    @pl.when(downward & turns_round)
-    def _():
-        pl.semaphore_signal(round_go, inc=1, device_id=round_source, device_id_type=MESH)
-
     @pl.when(upward & sends_round)
     def _():
-        pl.semaphore_signal(round_go, inc=1, device_id=round_turn, device_id_type=MESH)
         round_first().start()
 
     @pl.when(jnp.logical_not(sends_round))
@@ -329,6 +369,30 @@
             hop(0, j).start()
 
     hop(0, 1).start()
+
+    def go(i, who):
+        pl.semaphore_signal(goes.at[i], inc=1, device_id=who, device_id_type=MESH)
+
+    @pl.when(gives_go)
+    def _():
+        go(0, round_tell)
+
+    @pl.when(upward & turns_round)
+    def _():
+        go(0, round_tell_source)
+
+    @pl.when(downward & near_ahead)
+    def _():
+        go(1, relay_to)
+
+    @pl.when(gy == ny - 1)
+    def _():
+        go(2, y_up)
+
+    @pl.when(gy > 0)
+    def _():
+        go(2, y_down)
+
     with jax.named_scope("load_rest"):
         loads[1].wait()
     hop(0, 2).start()
@@ -339,8 +403,19 @@
     with jax.named_scope("starts"):
         near.start()
         z_start()
-        for j in range(3, chunks):
+        for j in range(3, chunks - late):
             hop(0, j).start()
+
+        @pl.when(jnp.logical_not(sends_straight))
+        def _():
+            for j in range(chunks - late, chunks):
+                hop(0, j).start()
+
+
+        @pl.when(gy < ny - 1)
+        def _():
+            pl.semaphore_wait(goes.at[2], jnp.where(gy == 0, 2, 1))
+
         for copy in y_copies:
             copy.start()
     with jax.named_scope("relay1"):
@@ -351,8 +426,15 @@
 
         @pl.when(downward & sends_round)
         def _():
-            pl.semaphore_wait(round_go, 1)
+            pl.semaphore_wait(goes.at[0], 1)
             round_first().start()
+
+    swaps = downward & (z_hi == bottom) & (gz == 1) & (chip_x == 0) & (gy == 0)
+    with jax.named_scope("relay3_first"):
+
+        @pl.when(swaps)
+        def _():
+            relay(3)
 
     with jax.named_scope("relay2"):
         relay(2)
@@ -360,7 +442,7 @@
 
         @pl.when(downward & turns_round)
         def _():
-            pl.semaphore_wait(round_go, 1)
+            pl.semaphore_wait(goes.at[0], 1)
 
         @pl.when(turns_round)
         def _():
@@ -370,7 +452,16 @@
     with jax.named_scope("z_pass_on"):
         z_pass_on()
     with jax.named_scope("relay3"):
-        relay(3)
+
+        @pl.when(jnp.logical_not(swaps))
+        def _():
+            relay(3)
+
+        @pl.when(sends_straight)
+        def _():
+            for j in range(chunks - late, chunks):
+                straight(j).start()
+
     with jax.named_scope("z_wait"):
         z_both.wait_recv()
     with jax.named_scope("z_sum"):
@@ -396,7 +487,7 @@
     with jax.named_scope("finish"):
         for j in range(chunks):
             arrival(j).wait_recv()
-            lax.fori_loop(j * per, (j + 1) * per, finish, 0)
+            lax.fori_loop(at_chunk[j], at_chunk[j + 1], finish, 0)
     with jax.named_scope("send_wait"):
         hop(0, 0).wait_send()
         for h in range(1, relays + 1):
@@ -409,7 +500,14 @@
         def _():
             round_last().wait_send()
 
-        rest = hold.at[:, pl.ds(detour * per, species - detour * per)]
+        for h in range(relays + 1):
+            end = hold.at[h, pl.ds(at_chunk[chunks - late], species - at_chunk[chunks - late])]
+
+            @pl.when(jnp.logical_not(misses(h)) if h else h == 0)
+            def _(h=h, end=end):
+                remote(end, end, late_send.at[h], far_recv.at[0], relay_to).wait_send()
+
+        rest = hold.at[:, pl.ds(at_chunk[1], at_chunk[chunks - late] - at_chunk[1])]
         remote(rest, rest, x_send, far_recv.at[0], relay_to).wait_send()
 
 
@@ -434,6 +532,7 @@
             pltpu.SemaphoreType.DMA,
             pltpu.SemaphoreType.DMA,
             pltpu.SemaphoreType.DMA((relays + 2,)),
+            pltpu.SemaphoreType.DMA((relays + 1,)),
             pltpu.SemaphoreType.DMA((relays, chunks)),
             pltpu.SemaphoreType.DMA,
             pltpu.SemaphoreType.DMA((chunks,)),
@@ -444,7 +543,7 @@
             pltpu.SemaphoreType.DMA((2,)),
             pltpu.SemaphoreType.DMA,
             pltpu.SemaphoreType.DMA((2,)),
-            pltpu.SemaphoreType.REGULAR,
+            pltpu.SemaphoreType.REGULAR((3,)),
         ],
         compiler_params=pltpu.CompilerParams(collective_id=0, has_side_effects=True),
     )(fields, strength)

time: 45.2 us -> 43.2 us (0.956)
  the two profiles are of different devices: /device:TPU:193 before, /device:TPU:40 now
where the time goes in v3:
time: 43.2 us; the launch traced here: 43.1 us
  Pallas kernels  42.1 us (97%)
  local copies, waits for them, and re-layouts  0.97 us (2%)
    pallas_call x1, Pallas kernels, local(): pl.pallas_call(functools.partial(kernel, sizes), out_shape=pltpu.VMEM(fie...  42.1 us
    unnamed x1, local copies, waits for them, and re-layouts  0.97 us

profile of v3, /device:TPU:40, one launch (start us, length us, event | category | flops | bytes accessed | tf_op | source)
XLA Modules:
  0.0 43.1 jit_solution(7234195706346595464)
XLA Ops:
  0.0 42.1 %shard_map.28 = f32[32,8,8,128]{3,2,1,0:T(8,128)S(1)} custom-call(f32[32,8,8,128]{3,2,1,0:T(8,128)} %fields.1, f32[32]{0:T(128)} %strength.1), custom_call_target="tpu_custom_call" | custom-call | tf_op jit(solution)/shard_map/pallas_call | solution.py:516
  42.1 1.0 %copy.4 = f32[32,8,8,128]{3,2,1,0:T(8,128)} copy(f32[32,8,8,128]{3,2,1,0:T(8,128)S(1)} %shard_map.28) | data formatting | bytes 2097152

commit v4 on v3

--- a/solution.py
+++ b/solution.py
@@ -16,9 +16,9 @@
 Z_GROUPS = 3
 sizes_of_chunks = (4, 4, 4, 4, 4, 4, 4, 4)
 chunks = len(sizes_of_chunks)
-late = 3
+late = 2
 relays = 3
-detour = 1
+detour = 3
 
 
 def tap_sum(tiles, length):
@@ -49,6 +49,7 @@
     scale_sem,
     x_send,
     detour_send,
+    second_send,
     late_send,
     hold_recv,
     detour_recv,
@@ -69,7 +70,7 @@
     at_chunk = [sum(sizes_of_chunks[:j]) for j in range(chunks + 1)]
     pairs = species // 2
     x_count = nx // (2 * Z_GROUPS)
-    first = at_chunk[2]
+    first = at_chunk[detour]
 
     gx = lax.axis_index("gx")
     gy = lax.axis_index("gy")
@@ -122,8 +123,11 @@
     bottom, middle, top = 0, Z_GROUPS - 2, Z_GROUPS - 1
     round_from = jnp.where(upward, top, bottom)
     round_to = top - round_from
-    sends_round = z_hi == round_from
-    turns_round = z_hi == middle
+    lifts = gz >= nz // 2
+    drops = (chip_x < x_count - 1) | (gy > 0) | (gz > 0)
+    goes_round = jnp.where(upward, drops, lifts)
+    sends_round = goes_round & (z_hi == round_from)
+    turns_round = goes_round & (z_hi == middle)
     beyond = wrap(chip_x + step, x_count) * Z_GROUPS
     round_mid = {"gx": (chip_x * Z_GROUPS + middle) * 2 + core}
     round_source = {"gx": (chip_x * Z_GROUPS + round_from) * 2 + core}
@@ -133,12 +137,19 @@
     round_help = {"gx": (beyond + round_to) * 2 + core}
     round_tell = {"gx": (wrap(chip_x - step, x_count) * Z_GROUPS + middle) * 2 + core}
     round_tell_source = {"gx": (chip_x * Z_GROUPS + bottom) * 2 + 1 - core}
+    round_beside = {"gx": (chip_x * Z_GROUPS + top) * 2 + 1 - core}
     gives_go = downward & (z_hi == top)
 
     def skips(h):
         below = jnp.where(gz < h, wrap(z_hi - 1, Z_GROUPS), z_hi)
         above = jnp.where(gz + h >= nz, wrap(z_hi + 1, Z_GROUPS), z_hi)
-        return jnp.where(upward, below, above) == round_from
+        lo = jnp.where(gz + h >= nz, gz + h - nz, gz + h)
+        from_lifted = (above == round_from) & (lo >= nz // 2)
+        dropped = (below == round_from) & ((chip_x < x_count - 1) | (gy > 0) | (gz != h))
+        return (upward & dropped) | (downward & from_lifted)
+
+    def skipped(h, j):
+        return skips(h) if j == 0 else downward & skips(h)
 
     sends_straight = upward & (z_hi == top) & (gz == nz - 1)
     gets_straight = downward & (z_hi == bottom) & (gz == nz - 1)
@@ -170,23 +181,26 @@
 
     @pl.when(upward & turns_round)
     def _():
-        greet(round_source)
+        greet(round_beside)
 
     @pl.when(downward & turns_round)
     def _():
         greet(round_help)
 
+    @pl.when(downward & (z_hi == bottom) & ((chip_x > 0) | (gy > 0) | (gz > 0)))
+    def _():
+        greet(round_turn)
+
     @pl.when(downward & sends_round)
     def _():
         greet(round_ask)
-        greet(round_turn)
 
     @pl.when(gets_straight)
     def _():
         greet(straight_from)
 
     also = jnp.where(sends_straight, 1, 0) + jnp.where(upward & near_behind, 1, 0) + jnp.where(gy == ny - 1, 2, jnp.where(gy > 0, 1, 0))
-    greeted = 3 + also + jnp.where(upward & turns_round, 2, jnp.where(gives_go | (upward & sends_round), 1, 0))
+    greeted = 3 + also + jnp.where(upward & turns_round, 1 + jnp.where(lifts, 1, 0), jnp.where(gives_go, jnp.where(drops, 1, 0) + jnp.where(lifts, 1, 0), 0))
 
     scale_copy = pltpu.make_async_copy(strength, scale, scale_sem)
     scale_copy.start()
@@ -207,7 +221,13 @@
 
     def hop(h, j):
         src = away(j) if h == 0 else hold.at[h - 1, part(j)]
-        send = detour_send.at[h] if j < detour else late_send.at[h] if j >= chunks - late else x_send
+        send = x_send
+        if j == 0:
+            send = detour_send.at[h]
+        elif j < detour:
+            send = second_send.at[h]
+        elif j >= chunks - late:
+            send = late_send.at[h]
         if h < relays:
             return remote(src, hold.at[h, part(j)], send, hold_recv.at[h, j], relay_to)
         return remote(src, xp.at[part(j), pl.ds(far_there, reach)], send, far_recv.at[j], last_to)
@@ -219,15 +239,20 @@
         dst = xp.at[part(j), pl.ds(far_there, reach)]
         return remote(away(j), dst, late_send.at[0], far_recv.at[j], straight_to)
 
-    around = part(0)
-
-    def round_first():
-        src = xp.at[around, pl.ds(reach + (cells - reach) * core, reach)]
-        return remote(src, hold.at[relays, around], detour_send.at[0], detour_recv, round_mid)
-
-    def round_last():
-        dst = xp.at[around, pl.ds(far_there, reach)]
-        return remote(hold.at[relays, around], dst, detour_send.at[relays + 1], far_recv.at[0], round_end)
+    def around(ups):
+        return pl.ds(0, at_chunk[detour if ups else 1])
+
+    def round_first(ups):
+        src = xp.at[around(ups), pl.ds(reach + (cells - reach) * core, reach)]
+        return remote(src, hold.at[relays, around(ups)], detour_send.at[0], detour_recv, round_mid)
+
+    def round_last(j):
+        dst = xp.at[part(j), pl.ds(far_there, reach)]
+        return remote(hold.at[relays, part(j)], dst, detour_send.at[relays + 1], far_recv.at[j], round_end)
+
+    def round_done(ups):
+        sent = hold.at[relays, around(ups)]
+        return remote(sent, sent, detour_send.at[relays + 1], far_recv.at[0], round_end)
 
     near = remote(
         xp.at[:, pl.ds(reach + (cells - reach) * (1 - core), reach)],
@@ -253,22 +278,19 @@
     def go_down(src, dst, recv):
         return remote(src, dst, z_send.at[1], recv, z_down)
 
-    def z_start():
-        @pl.when(downward & has_up)
-        def _():
-            pl.semaphore_wait(goes.at[1], 1)
-
+    def z_go_up():
         @pl.when(has_up)
         def _():
             go_up(z_last, z_before, z_recv).start()
 
+        @pl.when(gz == 0)
+        def _():
+            go_up(z_first, round_z.at[1], round_recv.at[1]).start()
+
+    def z_go_down():
         @pl.when(has_down)
         def _():
             go_down(z_first, z_after, z_recv).start()
-
-        @pl.when(gz == 0)
-        def _():
-            go_up(z_first, round_z.at[1], round_recv.at[1]).start()
 
         @pl.when(gz == nz - 1)
         def _():
@@ -339,7 +361,7 @@
         for j in range(chunks):
             if j < detour:
 
-                @pl.when(jnp.logical_not(skips(h)))
+                @pl.when(jnp.logical_not(skipped(h, j)))
                 def _(j=j):
                     hop(h - 1, j).wait_recv()
                     hop(h, j).start()
@@ -347,6 +369,13 @@
             elif j < chunks - late:
                 hop(h - 1, j).wait_recv()
                 hop(h, j).start()
+            if h == 2 and j == detour:
+
+                @pl.when(upward & turns_round)
+                def _():
+                    round_first(False).wait_recv()
+                    round_last(0).start()
+
 
         @pl.when(jnp.logical_not(misses(h)))
         def _():
@@ -359,25 +388,24 @@
     with jax.named_scope("barrier_wait"):
         pl.semaphore_wait(barrier, greeted)
 
-    @pl.when(upward & sends_round)
-    def _():
-        round_first().start()
-
-    @pl.when(jnp.logical_not(sends_round))
-    def _():
-        for j in range(detour):
+    for j in range(detour):
+
+        @pl.when(jnp.logical_not(skipped(0, j)))
+        def _(j=j):
             hop(0, j).start()
-
-    hop(0, 1).start()
 
     def go(i, who):
         pl.semaphore_signal(goes.at[i], inc=1, device_id=who, device_id_type=MESH)
 
-    @pl.when(gives_go)
+    @pl.when(gives_go & lifts)
     def _():
         go(0, round_tell)
 
-    @pl.when(upward & turns_round)
+    @pl.when(gives_go & drops)
+    def _():
+        go(0, partner)
+
+    @pl.when(upward & turns_round & lifts)
     def _():
         go(0, round_tell_source)
 
@@ -395,15 +423,20 @@
 
     with jax.named_scope("load_rest"):
         loads[1].wait()
-    hop(0, 2).start()
+    hop(0, detour).start()
     with jax.named_scope("z_turn"):
         lax.fori_loop(0, pairs, z_turn, 0, unroll=2)
     with jax.named_scope("y_turn"):
         lax.fori_loop(0, species, y_turn, 0, unroll=2)
     with jax.named_scope("starts"):
         near.start()
-        z_start()
-        for j in range(3, chunks - late):
+
+        @pl.when(upward)
+        def _():
+            z_go_up()
+
+        z_go_down()
+        for j in range(detour + 1, chunks - late):
             hop(0, j).start()
 
         @pl.when(jnp.logical_not(sends_straight))
@@ -411,6 +444,15 @@
             for j in range(chunks - late, chunks):
                 hop(0, j).start()
 
+        @pl.when(downward & has_up)
+        def _():
+            pl.semaphore_wait(goes.at[1], 1)
+            z_go_up()
+
+        @pl.when(upward & sends_round)
+        def _():
+            pl.semaphore_wait(goes.at[0], 1)
+            round_first(False).start()
 
         @pl.when(gy < ny - 1)
         def _():
@@ -427,7 +469,7 @@
         @pl.when(downward & sends_round)
         def _():
             pl.semaphore_wait(goes.at[0], 1)
-            round_first().start()
+            round_first(True).start()
 
     swaps = downward & (z_hi == bottom) & (gz == 1) & (chip_x == 0) & (gy == 0)
     with jax.named_scope("relay3_first"):
@@ -443,11 +485,9 @@
         @pl.when(downward & turns_round)
         def _():
             pl.semaphore_wait(goes.at[0], 1)
-
-        @pl.when(turns_round)
-        def _():
-            round_first().wait_recv()
-            round_last().start()
+            round_first(True).wait_recv()
+            for j in range(detour):
+                round_last(j).start()
 
     with jax.named_scope("z_pass_on"):
         z_pass_on()
@@ -473,32 +513,42 @@
     with jax.named_scope("near_wait"):
         near.wait()
         scale_copy.wait()
-    with jax.named_scope("sent_wait"):
-        y_both.wait_send()
-
-        @pl.when(has_up)
-        def _():
-            z_sent[0].wait_send()
-
-        @pl.when(has_down)
-        def _():
-            z_sent[1].wait_send()
-
     with jax.named_scope("finish"):
         for j in range(chunks):
             arrival(j).wait_recv()
             lax.fori_loop(at_chunk[j], at_chunk[j + 1], finish, 0)
+    with jax.named_scope("sides_wait"):
+        y_both.wait_send()
+
+        @pl.when(has_up)
+        def _():
+            z_sent[0].wait_send()
+
+        @pl.when(has_down)
+        def _():
+            z_sent[1].wait_send()
+
     with jax.named_scope("send_wait"):
-        hop(0, 0).wait_send()
-        for h in range(1, relays + 1):
-
-            @pl.when(jnp.logical_not(skips(h)))
+        for ups in (False, True):
+
+            @pl.when(sends_round & (downward if ups else upward))
+            def _(ups=ups):
+                round_first(ups).wait_send()
+
+            @pl.when(turns_round & (downward if ups else upward))
+            def _(ups=ups):
+                round_done(ups).wait_send()
+
+        for h in range(relays + 1):
+
+            @pl.when(jnp.logical_not(skipped(h, 0)))
             def _(h=h):
                 hop(h, 0).wait_send()
 
-        @pl.when(turns_round)
-        def _():
-            round_last().wait_send()
+            @pl.when(jnp.logical_not(skipped(h, 1)))
+            def _(h=h):
+                more = hold.at[h, pl.ds(at_chunk[1], at_chunk[detour] - at_chunk[1])]
+                remote(more, more, second_send.at[h], far_recv.at[0], relay_to).wait_send()
 
         for h in range(relays + 1):
             end = hold.at[h, pl.ds(at_chunk[chunks - late], species - at_chunk[chunks - late])]
@@ -507,7 +557,7 @@
             def _(h=h, end=end):
                 remote(end, end, late_send.at[h], far_recv.at[0], relay_to).wait_send()
 
-        rest = hold.at[:, pl.ds(at_chunk[1], at_chunk[chunks - late] - at_chunk[1])]
+        rest = hold.at[:, pl.ds(at_chunk[detour], at_chunk[chunks - late] - at_chunk[detour])]
         remote(rest, rest, x_send, far_recv.at[0], relay_to).wait_send()
 
 
@@ -533,6 +583,7 @@
             pltpu.SemaphoreType.DMA,
             pltpu.SemaphoreType.DMA((relays + 2,)),
             pltpu.SemaphoreType.DMA((relays + 1,)),
+            pltpu.SemaphoreType.DMA((relays + 1,)),
             pltpu.SemaphoreType.DMA((relays, chunks)),
             pltpu.SemaphoreType.DMA,
             pltpu.SemaphoreType.DMA((chunks,)),

time: 43.2 us -> 42.1 us (0.975)
  Pallas kernels: 42.1 us -> 41 us
    pallas_call x1, Pallas kernels: 42.1 us -> 41 us  [local(): pl.pallas_call(functools.partial(kernel, sizes), out_shape=pltpu.VMEM(fie...]
where the time goes in v4:
time: 42.1 us; the launch traced here: 42 us
  Pallas kernels  41 us (97%)
  local copies, waits for them, and re-layouts  0.97 us (2%)
    pallas_call x1, Pallas kernels, local(): pl.pallas_call(functools.partial(kernel, sizes), out_shape=pltpu.VMEM(fie...  41 us
    unnamed x1, local copies, waits for them, and re-layouts  0.97 us

profile of v4, /device:TPU:40, one launch (start us, length us, event | category | flops | bytes accessed | tf_op | source)
XLA Modules:
  0.0 42.0 jit_solution(12943140010729805414)
XLA Ops:
  0.0 41.0 %shard_map.28 = f32[32,8,8,128]{3,2,1,0:T(8,128)S(1)} custom-call(f32[32,8,8,128]{3,2,1,0:T(8,128)} %fields.1, f32[32]{0:T(128)} %strength.1), custom_call_target="tpu_custom_call" | custom-call | tf_op jit(solution)/shard_map/pallas_call | solution.py:566
  41.0 1.0 %copy.4 = f32[32,8,8,128]{3,2,1,0:T(8,128)} copy(f32[32,8,8,128]{3,2,1,0:T(8,128)S(1)} %shard_map.28) | data formatting | bytes 2097152

commit v5 on v4

--- a/solution.py
+++ b/solution.py
@@ -17,6 +17,7 @@
 sizes_of_chunks = (4, 4, 4, 4, 4, 4, 4, 4)
 chunks = len(sizes_of_chunks)
 late = 2
+straight_after = 3
 relays = 3
 detour = 3
 
@@ -151,13 +152,16 @@
     def skipped(h, j):
         return skips(h) if j == 0 else downward & skips(h)
 
-    sends_straight = upward & (z_hi == top) & (gz == nz - 1)
-    gets_straight = downward & (z_hi == bottom) & (gz == nz - 1)
+    straight_low = jnp.where((chip_x < x_count - 1) | (gy > 0), nz - 2, nz - 1)
+    sends_straight = upward & (z_hi == top) & (gz >= straight_low)
+    gets_straight = downward & (z_hi == bottom) & (gz >= jnp.where((chip_x > 0) | (gy > 0), nz - 2, nz - 1))
     straight_to = {"gx": (beyond + round_to) * 2 + 1 - core}
     straight_from = {"gx": (beyond + top) * 2 + 1 - core}
 
     def misses(h):
-        return upward & (z_hi == bottom) & (gz == h - 1)
+        hi = jnp.where(gz < h, wrap(z_hi - 1, Z_GROUPS), z_hi)
+        lo = jnp.where(gz < h, gz - h + nz, gz - h)
+        return upward & (hi == top) & (lo >= straight_low)
 
     barrier = pltpu.get_barrier_semaphore()
 
@@ -357,8 +361,18 @@
             out[s, x] = tiles[reach + x] + factor * (total[x] + acc[s, x])
         return 0
 
+    def go_straight():
+        for j in range(chunks - late, chunks):
+            straight(j).start()
+
     def relay(h):
         for j in range(chunks):
+            if h == 3 and j == straight_after:
+
+                @pl.when(sends_straight & (gz < nz - 1))
+                def _():
+                    go_straight()
+
             if j < detour:
 
                 @pl.when(jnp.logical_not(skipped(h, j)))
@@ -497,10 +511,9 @@
         def _():
             relay(3)
 
-        @pl.when(sends_straight)
-        def _():
-            for j in range(chunks - late, chunks):
-                straight(j).start()
+        @pl.when(sends_straight & (gz == nz - 1))
+        def _():
+            go_straight()
 
     with jax.named_scope("z_wait"):
         z_both.wait_recv()

time: 42.1 us -> 41.8 us (level)
  the two profiles are of different devices: /device:TPU:40 before, /device:TPU:192 now
where the time goes in v5:
time: 41.8 us; the launch traced here: 41.7 us
  Pallas kernels  40.7 us (97%)
  local copies, waits for them, and re-layouts  0.97 us (2%)
    pallas_call x1, Pallas kernels, local(): pl.pallas_call(functools.partial(kernel, sizes), out_shape=pltpu.VMEM(fie...  40.7 us
    unnamed x1, local copies, waits for them, and re-layouts  0.97 us

profile of v5, /device:TPU:192, one launch (start us, length us, event | category | flops | bytes accessed | tf_op | source)
XLA Modules:
  0.0 41.7 jit_solution(18405838025932766476)
XLA Ops:
  0.0 40.7 %shard_map.28 = f32[32,8,8,128]{3,2,1,0:T(8,128)S(1)} custom-call(f32[32,8,8,128]{3,2,1,0:T(8,128)} %fields.1, f32[32]{0:T(128)} %strength.1), custom_call_target="tpu_custom_call" | custom-call | tf_op jit(solution)/shard_map/pallas_call | solution.py:579
  40.7 1.0 %copy.4 = f32[32,8,8,128]{3,2,1,0:T(8,128)} copy(f32[32,8,8,128]{3,2,1,0:T(8,128)S(1)} %shard_map.28) | data formatting | bytes 2097152

commit v6 on v5

--- a/solution.py
+++ b/solution.py
@@ -526,12 +526,31 @@
     with jax.named_scope("near_wait"):
         near.wait()
         scale_copy.wait()
+    def wait_sent(h):
+        @pl.when(jnp.logical_not(skipped(h, 0)))
+        def _():
+            hop(h, 0).wait_send()
+
+        @pl.when(jnp.logical_not(skipped(h, 1)))
+        def _():
+            more = hold.at[h, pl.ds(at_chunk[1], at_chunk[detour] - at_chunk[1])]
+            remote(more, more, second_send.at[h], far_recv.at[0], relay_to).wait_send()
+
+        @pl.when(jnp.logical_not(misses(h)) if h else h == 0)
+        def _():
+            end = hold.at[h, pl.ds(at_chunk[chunks - late], species - at_chunk[chunks - late])]
+            remote(end, end, late_send.at[h], far_recv.at[0], relay_to).wait_send()
+
     with jax.named_scope("finish"):
         for j in range(chunks):
+            if j == chunks - 1:
+                for h in range(relays):
+                    if h:
+                        wait_sent(h)
+                y_both.wait_send()
             arrival(j).wait_recv()
             lax.fori_loop(at_chunk[j], at_chunk[j + 1], finish, 0)
-    with jax.named_scope("sides_wait"):
-        y_both.wait_send()
+    with jax.named_scope("send_wait"):
 
         @pl.when(has_up)
         def _():
@@ -541,7 +560,6 @@
         def _():
             z_sent[1].wait_send()
 
-    with jax.named_scope("send_wait"):
         for ups in (False, True):
 
             @pl.when(sends_round & (downward if ups else upward))
@@ -552,24 +570,8 @@
             def _(ups=ups):
                 round_done(ups).wait_send()
 
-        for h in range(relays + 1):
-
-            @pl.when(jnp.logical_not(skipped(h, 0)))
-            def _(h=h):
-                hop(h, 0).wait_send()
-
-            @pl.when(jnp.logical_not(skipped(h, 1)))
-            def _(h=h):
-                more = hold.at[h, pl.ds(at_chunk[1], at_chunk[detour] - at_chunk[1])]
-                remote(more, more, second_send.at[h], far_recv.at[0], relay_to).wait_send()
-
-        for h in range(relays + 1):
-            end = hold.at[h, pl.ds(at_chunk[chunks - late], species - at_chunk[chunks - late])]
-
-            @pl.when(jnp.logical_not(misses(h)) if h else h == 0)
-            def _(h=h, end=end):
-                remote(end, end, late_send.at[h], far_recv.at[0], relay_to).wait_send()
-
+        wait_sent(0)
+        wait_sent(relays)
         rest = hold.at[:, pl.ds(at_chunk[detour], at_chunk[chunks - late] - at_chunk[detour])]
         remote(rest, rest, x_send, far_recv.at[0], relay_to).wait_send()
 

time: 41.8 us -> 41.8 us (level)
  no operation moved by 1% of the time
where the time goes in v6:
time: 41.8 us; the launch traced here: 41.7 us
  Pallas kernels  40.7 us (97%)
  local copies, waits for them, and re-layouts  0.97 us (2%)
    pallas_call x1, Pallas kernels, local(): pl.pallas_call(functools.partial(kernel, sizes), out_shape=pltpu.VMEM(fie...  40.7 us
    unnamed x1, local copies, waits for them, and re-layouts  0.97 us

profile of v6, /device:TPU:192, one launch (start us, length us, event | category | flops | bytes accessed | tf_op | source)
XLA Modules:
  0.0 41.7 jit_solution(600924084448320032)
XLA Ops:
  0.0 40.7 %shard_map.28 = f32[32,8,8,128]{3,2,1,0:T(8,128)S(1)} custom-call(f32[32,8,8,128]{3,2,1,0:T(8,128)} %fields.1, f32[32]{0:T(128)} %strength.1), custom_call_target="tpu_custom_call" | custom-call | tf_op jit(solution)/shard_map/pallas_call | solution.py:581
  40.7 1.0 %copy.4 = f32[32,8,8,128]{3,2,1,0:T(8,128)} copy(f32[32,8,8,128]{3,2,1,0:T(8,128)S(1)} %shard_map.28) | data formatting | bytes 2097152

commit v7 on v6

--- a/solution.py
+++ b/solution.py
@@ -48,10 +48,8 @@
     scale,
     load_sem,
     scale_sem,
-    x_send,
+    sent,
     detour_send,
-    second_send,
-    late_send,
     hold_recv,
     detour_recv,
     far_recv,
@@ -68,6 +66,7 @@
     species = xp.shape[0]
     cells = fields.shape[1]
     assert sum(sizes_of_chunks) == species
+    assert sum(sizes_of_chunks[1:detour]) == sum(sizes_of_chunks[-late:])
     at_chunk = [sum(sizes_of_chunks[:j]) for j in range(chunks + 1)]
     pairs = species // 2
     x_count = nx // (2 * Z_GROUPS)
@@ -225,23 +224,23 @@
 
     def hop(h, j):
         src = away(j) if h == 0 else hold.at[h - 1, part(j)]
-        send = x_send
+        send = sent.at[relays + 1]
         if j == 0:
             send = detour_send.at[h]
         elif j < detour:
-            send = second_send.at[h]
+            send = sent.at[jnp.where(upward, relays + 1, h)]
         elif j >= chunks - late:
-            send = late_send.at[h]
+            send = sent.at[jnp.where(upward, h, relays + 1)]
         if h < relays:
             return remote(src, hold.at[h, part(j)], send, hold_recv.at[h, j], relay_to)
         return remote(src, xp.at[part(j), pl.ds(far_there, reach)], send, far_recv.at[j], last_to)
 
     def arrival(j):
-        return remote(hold.at[0, part(j)], xp.at[part(j), pl.ds(far_here, reach)], x_send, far_recv.at[j], last_to)
+        return remote(hold.at[0, part(j)], xp.at[part(j), pl.ds(far_here, reach)], sent.at[relays + 1], far_recv.at[j], last_to)
 
     def straight(j):
         dst = xp.at[part(j), pl.ds(far_there, reach)]
-        return remote(away(j), dst, late_send.at[0], far_recv.at[j], straight_to)
+        return remote(away(j), dst, sent.at[0], far_recv.at[j], straight_to)
 
     def around(ups):
         return pl.ds(0, at_chunk[detour if ups else 1])
@@ -255,8 +254,8 @@
         return remote(hold.at[relays, part(j)], dst, detour_send.at[relays + 1], far_recv.at[j], round_end)
 
     def round_done(ups):
-        sent = hold.at[relays, around(ups)]
-        return remote(sent, sent, detour_send.at[relays + 1], far_recv.at[0], round_end)
+        done = hold.at[relays, around(ups)]
+        return remote(done, done, detour_send.at[relays + 1], far_recv.at[0], round_end)
 
     near = remote(
         xp.at[:, pl.ds(reach + (cells - reach) * (1 - core), reach)],
@@ -531,15 +530,10 @@
         def _():
             hop(h, 0).wait_send()
 
-        @pl.when(jnp.logical_not(skipped(h, 1)))
-        def _():
-            more = hold.at[h, pl.ds(at_chunk[1], at_chunk[detour] - at_chunk[1])]
-            remote(more, more, second_send.at[h], far_recv.at[0], relay_to).wait_send()
-
-        @pl.when(jnp.logical_not(misses(h)) if h else h == 0)
-        def _():
-            end = hold.at[h, pl.ds(at_chunk[chunks - late], species - at_chunk[chunks - late])]
-            remote(end, end, late_send.at[h], far_recv.at[0], relay_to).wait_send()
+        @pl.when(jnp.logical_not(misses(h) | skipped(h, 1) if h else skipped(h, 1)))
+        def _():
+            some = hold.at[h, pl.ds(0, at_chunk[detour] - at_chunk[1])]
+            remote(some, some, sent.at[h], far_recv.at[0], relay_to).wait_send()
 
     with jax.named_scope("finish"):
         for j in range(chunks):
@@ -572,8 +566,8 @@
 
         wait_sent(0)
         wait_sent(relays)
-        rest = hold.at[:, pl.ds(at_chunk[detour], at_chunk[chunks - late] - at_chunk[detour])]
-        remote(rest, rest, x_send, far_recv.at[0], relay_to).wait_send()
+        rest = hold.at[:, pl.ds(0, at_chunk[chunks - late] - at_chunk[1])]
+        remote(rest, rest, sent.at[relays + 1], far_recv.at[0], relay_to).wait_send()
 
 
 def local(sizes, fields, strength):
@@ -595,10 +589,8 @@
             pltpu.SMEM((species,), jnp.float32),
             pltpu.SemaphoreType.DMA((2,)),
             pltpu.SemaphoreType.DMA,
-            pltpu.SemaphoreType.DMA,
             pltpu.SemaphoreType.DMA((relays + 2,)),
-            pltpu.SemaphoreType.DMA((relays + 1,)),
-            pltpu.SemaphoreType.DMA((relays + 1,)),
+            pltpu.SemaphoreType.DMA((relays + 2,)),
             pltpu.SemaphoreType.DMA((relays, chunks)),
             pltpu.SemaphoreType.DMA,
             pltpu.SemaphoreType.DMA((chunks,)),

time: 41.8 us -> 41.8 us (level)
  no operation moved by 1% of the time
where the time goes in v7:
time: 41.8 us; the launch traced here: 41.6 us
  Pallas kernels  40.7 us (97%)
  local copies, waits for them, and re-layouts  0.97 us (2%)
    pallas_call x1, Pallas kernels, local(): pl.pallas_call(functools.partial(kernel, sizes), out_shape=pltpu.VMEM(fie...  40.7 us
    unnamed x1, local copies, waits for them, and re-layouts  0.97 us

profile of v7, /device:TPU:192, one launch (start us, length us, event | category | flops | bytes accessed | tf_op | source)
XLA Modules:
  0.0 41.6 jit_solution(10842763183440790526)
XLA Ops:
  0.0 40.7 %shard_map.28 = f32[32,8,8,128]{3,2,1,0:T(8,128)S(1)} custom-call(f32[32,8,8,128]{3,2,1,0:T(8,128)} %fields.1, f32[32]{0:T(128)} %strength.1), custom_call_target="tpu_custom_call" | custom-call | tf_op jit(solution)/shard_map/pallas_call | solution.py:575
  40.7 1.0 %copy.4 = f32[32,8,8,128]{3,2,1,0:T(8,128)} copy(f32[32,8,8,128]{3,2,1,0:T(8,128)S(1)} %shard_map.28) | data formatting | bytes 2097152
